TPU v7x, 32 devices: a whole 2x2x4 slice. The times are simulated.
32 devices in a mesh: pair: 4 (over z), aux: 8 (over y, x, core).
Axes of the slice: x: 2, y: 2, z: 4, core: 2. Of those that a mesh axis runs over, the one named last changes fastest.
Arguments:
- integrals: bfloat16 [12288, 12288], P('pair', 'aux'), may hold values from -0.1875 to 0.1875
- energy_gaps: float32 [12288], P('pair'), may hold values from 0.3 to 3
- trial_vectors: float32 [12288, 64], P('pair'), may hold values from -160 to 160
Outputs:
- sigma_vectors: float32 [12288, 64], P(('pair', 'aux'))
- subspace: float32 [64, 64], replicated
- residuals: float32 [12288, 64], P(('pair', 'aux'))
- residual_norms: float32 [64], replicated
All inputs are finite; a program needn't handle non-finite values.
Results may differ from a plain program's by a relative error of at most 0.0052.
Values may be sent and summed in bfloat16 or wider, within the bound.
A program may use at most 64 MiB of HBM per device.

v0:
```python
import jax
import jax.numpy as jnp
from jax import lax
from jax.sharding import PartitionSpec as P

epsilon = 1e-06


def local(integrals, energy_gaps, trial_vectors):
    pair_rows = trial_vectors.shape[0]
    row_share = pair_rows // lax.axis_size("aux")
    total_pairs = float(pair_rows * lax.axis_size("pair"))
    trial_half = trial_vectors.astype(jnp.bfloat16)
    partial_value = lax.dot_general(
        integrals, trial_half, (((0,), (0,)), ((), ())), preferred_element_type=jnp.float32
    )
    aux_half = lax.psum(partial_value, "pair").astype(jnp.bfloat16)
    coupled = lax.psum_scatter(
        jnp.dot(integrals, aux_half, preferred_element_type=jnp.float32),
        "aux",
        scatter_dimension=0,
        tiled=True,
    )
    first_own = lax.axis_index("aux") * row_share
    own_trial = lax.dynamic_slice_in_dim(trial_vectors, first_own, row_share, 0)
    own_gaps = lax.dynamic_slice_in_dim(energy_gaps, first_own, row_share, 0)
    sigma_rows = own_gaps[:, None] * own_trial + 2.0 * coupled
    products = lax.dot_general(
        own_trial,
        sigma_rows,
        (((0,), (0,)), ((), ())),
        precision=lax.Precision.HIGHEST,
        preferred_element_type=jnp.float32,
    )
    squares = jnp.sum(own_trial * own_trial, axis=0)
    sigma_sq = jnp.sum(sigma_rows * sigma_rows, axis=0)
    products, squares, sigma_sq = lax.psum((products, squares, sigma_sq), ("pair", "aux"))
    subspace = products / total_pairs
    rayleigh = jnp.diagonal(subspace) / (squares / total_pairs + epsilon)
    residual_rows = sigma_rows - own_trial * rayleigh[None, :]
    residual_sq = sigma_sq - 2.0 * rayleigh * jnp.diagonal(products) + rayleigh * rayleigh * squares
    residual_norms = jnp.sqrt(residual_sq / total_pairs + epsilon)
    return (sigma_rows, subspace, residual_rows, residual_norms)


def solution(mesh):
    return jax.shard_map(
        local,
        mesh=mesh,
        in_specs=(P("pair", "aux"), P("pair"), P("pair", None)),
        out_specs=(P(("pair", "aux"), None), P(), P(("pair", "aux"), None), P()),
        check_vma=False,
    )
```

profile of v0, /device:TPU:0, one launch (start us, length us, event | category | flops | bytes accessed | tf_op | source)
XLA Modules:
  0.0 144.5 jit_solution(822502268813856229)
XLA Ops:
  7.2 0.0 reduce-scatter.2.cloned.1.call-start
  7.2 5.5 %fusion.1 = f32[1536,64]{1,0:T(8,128)S(1)} fusion(bf16[3072,1536]{1,0:T(8,128)(2,1)} %param.3, f32[3072,64]{0,1:T(8,128)} %param.5), kind=kOutput, calls=%fused_computation.4 | convolution fusion | flops 604176384 | bytes 10616832 | tf_op jit(solution)/shard_map/dot_general | solution.py:14
  12.7 37.3 %all-reduce.2 = bf16[1536,64]{1,0:T(8,128)(2,1)S(1)} all-reduce(f32[1536,64]{1,0:T(8,128)S(1)} %fusion.1), channel_id=1, replica_groups=mesh['pair'=4,'aux'=8] {'pair'}, use_global_device_ids=true, to_apply=%region_0.0 | all-reduce | flops 98304 | bytes 589824 | tf_op jit(solution)/shard_map/psum | solution.py:17
  50.0 7.5 %convolution_bitcast_fusion = f32[3072,64]{0,1:T(8,128)} fusion(bf16[3072,1536]{1,0:T(8,128)(2,1)} %param.3, bf16[1536,64]{1,0:T(8,128)(2,1)S(1)} %all-reduce.2), kind=kOutput, calls=%fused_computation.2 | convolution fusion | flops 603979776 | bytes 10420224 | tf_op jit(solution)/shard_map/dot_general | solution.py:19
  57.5 0.0 reduce-scatter.2.cloned.1.call-update
  57.5 0.8 dynamic_slice.6
  58.3 33.7 %reduce-scatter.2.cloned.1.call-done = f32[384,64]{0,1:T(8,128)} async-done(((f32[3072,64]{0,1:T(8,128)}), f32[384,64]{0,1:T(8,128)}) %reduce-scatter.2.cloned.1.call-update) | async-done | bytes 98320 | tf_op jit(solution)/shard_map/reduce_scatter | solution.py:18
  92.0 1.1 multiply_reduce_fusion
  93.1 0.0 copy-start.1
  93.1 1.2 fusion.3
  94.3 39.6 %all-reduce = (f32[64,64]{1,0:T(8,128)S(1)}, f32[64]{0:T(128)S(1)}, f32[64]{0:T(128)S(1)}) all-reduce(f32[64,64]{1,0:T(8,128)S(1)} %fusion.3, f32[64]{0:T(128)S(1)} %get-tuple-element.11, f32[64]{0:T(128)S(1)} %get-tuple-element.9), channel_id=1, replica_groups=mesh['pair'=4,'aux'=8] {'pair','aux'}, use_global_device_ids=true, to_apply=%region_2.0 | all-reduce | flops 4224 | bytes 33792 | tf_op jit(solution)/shard_map/psum | solution.py:37
  133.9 0.0 copy-start
  133.9 0.8 gather_fusion.1
  134.7 0.8 gather_fusion
  135.5 0.5 add_sqrt_fusion
  136.1 1.6 %multiply_subtract_fusion = f32[384,64]{0,1:T(8,128)} fusion(f32[384,64]{0,1:T(8,128)S(1)} %get-tuple-element.10, f32[3072,64]{0,1:T(8,128)} %param.5, s32[]{:T(128)S(6)} %select_n.10, f32[64]{0:T(128)S(1)} %get-tuple-element.8), kind=kLoop, calls=%fused_computation.7 | loop fusion | flops 49152 | bytes 295172 | tf_op jit(solution)/shard_map/sub | solution.py:40
  137.7 0.0 copy-done.1
  137.7 0.0 copy-done
  (2 shorter events, 0.0 us)
Async XLA Ops:
  7.2 84.8 %reduce-scatter.2.cloned.1.call-start = ((), (), s32[]{:S(2)}) async-start(), calls=%async_computation.1 | async-start | bytes 884736 | tf_op jit(solution)/shard_map/reduce_scatter | solution.py:18
  93.1 44.6 %copy-start.1 = (f32[384,64]{0,1:T(8,128)}, f32[384,64]{0,1:T(8,128)S(1)}, u32[]{:S(2)}) copy-start(f32[384,64]{0,1:T(8,128)S(1)} %get-tuple-element.10) | copy-start | bytes 294916
  133.9 3.8 %copy-start = (f32[64,64]{1,0:T(8,128)}, f32[64,64]{1,0:T(8,128)S(1)}, u32[]{:S(2)}) copy-start(f32[64,64]{1,0:T(8,128)S(1)} %broadcast_multiply_fusion) | copy-start | bytes 49156
Sparse Core Ops, SparseCore 0:
  57.6 34.3 reduce-scatter.1
where the time goes:
time: 145 us
  blocking collectives  76.9 us (53%)
  waiting for transfers between devices  33.7 us (23%)
  matrix products  14.2 us (10%)
  between operations  14.1 us (10%)
  other arithmetic  3.22 us (2%)
  local copies, waits for them, and re-layouts  2.41 us (2%)
    psum x1, blocking collectives, local(): lax.psum((products, squares, sigma_sq), ('pair', 'aux'))  39.6 us
    psum x1, blocking collectives, local(): aux_half = lax.psum(partial_value, 'pair').astype(jnp.bfloat16)  37.3 us
    reduce_scatter x1, waiting for transfers between devices, local(): lax.psum_scatter(jnp.dot(integrals, aux_half, preferred_element_type=jnp....  33.7 us
    dot_general x1, matrix products, local(): jnp.dot(integrals, aux_half, preferred_element_type=jnp.float32)  7.53 us
    dot_general x1, matrix products, local(): lax.dot_general(integrals, trial_half, (((0,), (0,)), ((), ())), preferre...  5.45 us
  transfers between devices with their start and end apart: 1, of which 1 were waited for; matrix products, arithmetic and copies ran while one was open for 1% of the time, Pallas kernels for 0%

commit v1 on v0

v1 whole, which is shorter than its diff:
```python
import functools

import jax
import jax.numpy as jnp
from jax import lax
from jax.experimental import pallas as pl
from jax.experimental.pallas import tpu as pltpu
from jax.sharding import PartitionSpec as P

epsilon = 1e-06
MESH = pl.DeviceIdType.MESH
f32, bf16 = jnp.float32, jnp.bfloat16
LAG = 2
NT = (((1,), (1,)), ((), ()))


def exact(a, b):
    return lax.dot_general(a, b, NT, precision=lax.Precision.HIGHEST, preferred_element_type=f32)


def kernel(
    np_, na, chunks, width, share,
    ints_hbm, gaps_hbm, trial_hbm,
    sigma_hbm, sub_hbm, res_hbm, norm_hbm,
    ints, gaps, trial, half, own, acc, mat, gram,
    pre_in, pre_out, suf_in, suf_out,
    b1_out, b1_in, b2_out, b2_in,
    m1_out, m1_in, m2, m3, n1, n2,
    sigma, sub, res, norm,
    load, aload, pre_s, pre_r, suf_s, suf_r,
    b1_s, b1_r, b2_s, b2_r, m1_s, m1_r, m2_s, m2_r, m3_s, m3_r, n1_s, n1_r, n2_s, n2_r, store,
):
    z, a = lax.axis_index("pair"), lax.axis_index("aux")
    core, chip, chips = a % 2, a // 2, na // 2
    vecs = trial.shape[0]

    trial_load = pltpu.make_async_copy(trial_hbm, trial, aload.at[0])
    gaps_load = pltpu.make_async_copy(gaps_hbm, gaps, aload.at[1])
    trial_load.start()
    loads = [
        pltpu.make_async_copy(ints_hbm.at[:, pl.ds(c * width, width)], ints.at[c], load.at[c])
        for c in range(chunks)
    ]
    loads[0].start()
    gaps_load.start()
    for c in range(1, chunks):
        loads[c].start()

    barrier = pltpu.get_barrier_semaphore()
    for d in range(1, np_):
        pl.semaphore_signal(barrier, inc=1, device_id={"pair": (z + d) % np_, "aux": a}, device_id_type=MESH)
    for d in range(1, na):
        pl.semaphore_signal(barrier, inc=1, device_id={"pair": z, "aux": (a + d) % na}, device_id_type=MESH)

    def remote(src, dst, s, r, pair, aux):
        return pltpu.make_async_remote_copy(
            src_ref=src, dst_ref=dst, send_sem=s, recv_sem=r,
            device_id={"pair": pair, "aux": aux}, device_id_type=MESH,
        )

    def prefix(c):
        return remote(pre_out.at[c], pre_in.at[c], pre_s.at[c], pre_r.at[c], z + 1, a)

    def suffix(c):
        return remote(suf_out.at[c], suf_in.at[c], suf_s.at[c], suf_r.at[c], z - 1, a)

    acc[...] = jnp.zeros_like(acc)
    mat[...] = jnp.zeros_like(mat)
    trial_load.wait()
    half[...] = trial[...].astype(bf16)
    gaps_load.wait()
    first = pl.multiple_of(a * share, 128)
    rows = share // 128

    def own_trial():
        return trial[:, pl.ds(first, share)]

    def own_gaps():
        return jnp.concatenate([gaps[pl.ds(a * rows + q, 1), :] for q in range(rows)], axis=1)

    eye = lax.broadcasted_iota(jnp.int32, (vecs, vecs), 0) == lax.broadcasted_iota(jnp.int32, (vecs, vecs), 1)

    def as_row(column):
        return jnp.sum(jnp.where(eye, column, 0.0), axis=0, keepdims=True)

    mine = own_trial()
    gram[...] = exact(mine, mine * own_gaps())
    pl.semaphore_wait(barrier, np_ - 1 + na - 1)

    after = np_ - 1 - z
    longest = jnp.maximum(z, after)

    def step(t, carry):
        @pl.when(t < chunks)
        def _():
            pltpu.make_async_copy(ints_hbm.at[:, pl.ds(0, width)], ints.at[t], load.at[t]).wait()
            own[t] = jnp.dot(half[...], ints[t], preferred_element_type=f32)

        p = t - LAG * z

        @pl.when((p >= 0) & (p < chunks) & (after > 0))
        def _():
            @pl.when(z == 0)
            def _():
                pre_out[p] = own[p].astype(bf16)

            @pl.when(z > 0)
            def _():
                prefix(p).wait_recv()
                pre_out[p] = (own[p] + pre_in[p].astype(f32)).astype(bf16)

            prefix(p).start()

        s = t - LAG * after

        @pl.when((s >= 0) & (s < chunks) & (z > 0))
        def _():
            @pl.when(after == 0)
            def _():
                suf_out[s] = own[s].astype(bf16)

            @pl.when(after > 0)
            def _():
                suffix(s).wait_recv()
                suf_out[s] = (own[s] + suf_in[s].astype(f32)).astype(bf16)

            suffix(s).start()

        c = t - LAG * longest

        @pl.when((c >= 0) & (c < chunks))
        def _():
            @pl.when(z == np_ - 1)
            def _():
                prefix(c).wait_recv()

            @pl.when(z == 0)
            def _():
                suffix(c).wait_recv()

            @pl.when(z > 0)
            def _():
                own[c] = own[c] + pre_in[c].astype(f32)

            @pl.when(after > 0)
            def _():
                own[c] = own[c] + suf_in[c].astype(f32)

            aux = own[c].astype(bf16)
            for b in range(chips):
                part = lax.dot_general(
                    aux, ints[c, pl.ds(b * 2 * share, 2 * share), :], NT, preferred_element_type=f32
                )
                acc[2 * b] += part[:, :share]
                acc[2 * b + 1] += part[:, share:]

            @pl.when(c % np_ == z)
            def _():
                total = own[c]
                mat[...] += exact(total, total.astype(bf16).astype(f32))

        return carry

    lax.fori_loop(0, chunks + LAG * (np_ - 1), step, 0)

    other = chip * 2 + 1 - core
    pending = []
    product = gram[...] + 2.0 * mat[...]
    mine = own_trial()
    squares = as_row(jnp.sum(mine * mine, axis=1, keepdims=True))
    h = vecs // 2
    m1_out[0:h] = jnp.concatenate([product[:h], product[h:]], axis=1)
    m1_out[h:] = jnp.broadcast_to(jnp.concatenate([squares, squares], axis=1), (8, 2 * vecs))
    m1_copy = remote(m1_out, m1_in, m1_s, m1_r, z, other)
    m1_copy.start()
    pending.append(m1_copy)

    b1 = []
    for d in range(chips):
        j = (chip + 1 + d) % chips
        b1_out[d] = acc[2 * j + 1 - core].astype(bf16)
        copy = remote(b1_out.at[d], b1_in.at[d], b1_s.at[d], b1_r.at[d], z, other)
        copy.start()
        b1.append(copy)
        pending.append(copy)
    m1_copy.wait_recv()
    m2[chip] = m1_out[...] + m1_in[...]
    for d in range(1, chips):
        copy = remote(m2.at[chip], m2.at[chip], m2_s.at[d], m2_r.at[chip], z, ((chip + d) % chips) * 2 + core)
        copy.start()
        pending.append(copy)
    for d in range(chips - 1):
        j = (chip + 1 + d) % chips
        b1[d].wait_recv()
        b2_out[d] = (acc[2 * j + core] + b1_in[d].astype(f32)).astype(bf16)
        copy = remote(b2_out.at[d], b2_in.at[d], b2_s.at[d], b2_r.at[d], z, 2 * j + core)
        copy.start()
        pending.append(copy)
    b1[chips - 1].wait_recv()
    coupled = acc[a] + b1_in[chips - 1].astype(f32)

    for d in range(1, chips):
        j = (chip + d) % chips
        remote(m2.at[j], m2.at[j], m2_s.at[d], m2_r.at[j], z, a).wait_recv()
    total = m2[0]
    for j in range(1, chips):
        total = total + m2[j]
    m3[z] = total
    for d in range(1, np_):
        copy = remote(m3.at[z], m3.at[z], m3_s.at[d], m3_r.at[z], (z + d) % np_, a)
        copy.start()
        pending.append(copy)

    for d in range(chips - 1):
        remote(b2_out.at[d], b2_in.at[d], b2_s.at[d], b2_r.at[d], z, a).wait_recv()
        coupled = coupled + b2_in[d].astype(f32)
    mine = own_trial()
    values = own_gaps() * mine + 2.0 * coupled
    sigma[...] = values
    lane = lax.broadcasted_iota(jnp.int32, (vecs, 128), 1)
    sums = jnp.where(
        lane == 0,
        jnp.sum(values * values, axis=1, keepdims=True),
        jnp.where(lane == 1, jnp.sum(values * mine, axis=1, keepdims=True), 0.0),
    )
    n1[a] = jnp.transpose(sums)[:8]
    for d in range(1, na):
        copy = remote(n1.at[a], n1.at[a], n1_s.at[d], n1_r.at[a], z, (a + d) % na)
        copy.start()
        pending.append(copy)
    outs = [pltpu.make_async_copy(sigma, sigma_hbm, store.at[0])]
    outs[0].start()
    for d in range(1, na):
        j = (a + d) % na
        remote(n1.at[j], n1.at[j], n1_s.at[d], n1_r.at[j], z, j).wait_recv()
    sums = n1[0]
    for j in range(1, na):
        sums = sums + n1[j]
    n2[z] = sums
    for d in range(1, np_):
        copy = remote(n2.at[z], n2.at[z], n2_s.at[d], n2_r.at[z], (z + d) % np_, a)
        copy.start()
        pending.append(copy)

    for d in range(1, np_):
        j = (z + d) % np_
        remote(m3.at[j], m3.at[j], m3_s.at[d], m3_r.at[j], j, a).wait_recv()
    total = m3[0]
    for j in range(1, np_):
        total = total + m3[j]
    pairs = float(np_ * na * share)
    subspace = jnp.concatenate([total[:h, :vecs], total[:h, vecs:]], axis=0) / pairs
    sub[...] = subspace
    outs.append(pltpu.make_async_copy(sub, sub_hbm, store.at[1]))
    outs[1].start()
    squares = total[h:h + 1, :vecs]
    diagonal = jnp.sum(jnp.where(eye, subspace, 0.0), axis=0, keepdims=True)
    rayleigh = diagonal / (squares / pairs + epsilon)
    column = jnp.sum(jnp.where(eye, rayleigh, 0.0), axis=1, keepdims=True)
    res[...] = sigma[...] - own_trial() * column
    outs.append(pltpu.make_async_copy(res, res_hbm, store.at[2]))
    outs[2].start()

    for d in range(1, np_):
        j = (z + d) % np_
        remote(n2.at[j], n2.at[j], n2_s.at[d], n2_r.at[j], j, a).wait_recv()
    sums = n2[0]
    for j in range(1, np_):
        sums = sums + n2[j]
    residual_sq = sums[0:1] - 2.0 * rayleigh * sums[1:2] + rayleigh * rayleigh * squares
    norm[...] = jnp.sqrt(residual_sq / pairs + epsilon)
    outs.append(pltpu.make_async_copy(norm, norm_hbm, store.at[3]))
    outs[3].start()

    @pl.when(after > 0)
    def _():
        for c in range(chunks):
            prefix(c).wait_send()

    @pl.when(z > 0)
    def _():
        for c in range(chunks):
            suffix(c).wait_send()

    for copy in pending:
        copy.wait_send()
    for copy in outs:
        copy.wait()


def solution(mesh):
    np_, na = mesh.shape["pair"], mesh.shape["aux"]
    chips = na // 2

    def local(integrals, energy_gaps, trial_vectors):
        rows, cols = integrals.shape
        vecs = trial_vectors.shape[1]
        width = 256
        chunks, share = cols // width, rows // na
        anywhere = pl.BlockSpec(memory_space=pl.ANY)
        dma = pltpu.SemaphoreType.DMA
        message = (vecs // 2 + 8, 2 * vecs)
        sigma, subspace, residuals, norms = pl.pallas_call(
            functools.partial(kernel, np_, na, chunks, width, share),
            out_shape=[
                jax.ShapeDtypeStruct((vecs, share), f32),
                jax.ShapeDtypeStruct((vecs, vecs), f32),
                jax.ShapeDtypeStruct((vecs, share), f32),
                jax.ShapeDtypeStruct((1, vecs), f32),
            ],
            in_specs=[pl.BlockSpec(memory_space=pltpu.HBM)] * 3,
            out_specs=[anywhere] * 4,
            scratch_shapes=[
                pltpu.VMEM((chunks, rows, width), bf16),
                pltpu.VMEM((rows // 128, 128), f32),
                pltpu.VMEM((vecs, rows), f32),
                pltpu.VMEM((vecs, rows), bf16),
                pltpu.VMEM((chunks, vecs, width), f32),
                pltpu.VMEM((na, vecs, share), f32),
                pltpu.VMEM((vecs, vecs), f32),
                pltpu.VMEM((vecs, vecs), f32),
                *[pltpu.VMEM((chunks, vecs, width), bf16)] * 4,
                *[pltpu.VMEM((chips, vecs, share), bf16)] * 4,
                pltpu.VMEM(message, f32),
                pltpu.VMEM(message, f32),
                pltpu.VMEM((chips,) + message, f32),
                pltpu.VMEM((np_,) + message, f32),
                pltpu.VMEM((na, 8, vecs), f32),
                pltpu.VMEM((np_, 8, vecs), f32),
                pltpu.VMEM((vecs, share), f32),
                pltpu.VMEM((vecs, vecs), f32),
                pltpu.VMEM((vecs, share), f32),
                pltpu.VMEM((1, vecs), f32),
                dma((chunks,)), dma((2,)),
                dma((chunks,)), dma((chunks,)), dma((chunks,)), dma((chunks,)),
                dma((chips,)), dma((chips,)), dma((chips,)), dma((chips,)),
                dma, dma, dma((chips,)), dma((chips,)),
                dma((np_,)), dma((np_,)), dma((na,)), dma((na,)), dma((np_,)), dma((np_,)),
                dma((4,)),
            ],
            compiler_params=pltpu.CompilerParams(
                collective_id=0, has_side_effects=True, vmem_limit_bytes=40 * 1024 * 1024
            ),
            name="sigma_build",
        )(integrals, energy_gaps.reshape(rows // 128, 128), trial_vectors.T)
        return sigma.T, subspace, residuals.T, norms.reshape(vecs)

    return jax.shard_map(
        local,
        mesh=mesh,
        in_specs=(P("pair", "aux"), P("pair"), P("pair", None)),
        out_specs=(P(("pair", "aux"), None), P(), P(("pair", "aux"), None), P()),
        check_vma=False,
    )
```

time: 145 us -> 44.7 us (0.31)
  blocking collectives: 76.9 us -> 0 us
  Pallas kernels: 0 us -> 35.8 us
  waiting for transfers between devices: 33.7 us -> 0 us
  matrix products: 14.2 us -> 0 us
  between operations: 14.1 us -> 0.65 us
  local copies, waits for them, and re-layouts: 2.41 us -> 7.92 us
  other arithmetic: 3.22 us -> 0 us
    psum x2 -> x0, blocking collectives: 76.9 us -> none  [the longest x1 39.6 us: local(): lax.psum((products, squares, sigma_sq), ('pair', 'aux'))]
    pallas_call x0 -> x1, Pallas kernels: none -> 35.8 us  [local(): pl.pallas_call(functools.partial(kernel, np_, na, chunks, width, share),...]
    reduce_scatter x1 -> x0, waiting for transfers between devices: 33.7 us -> none  [local(): lax.psum_scatter(jnp.dot(integrals, aux_half, preferred_element_type=jnp....]
    dot_general x3 -> x0, matrix products: 14.2 us -> none  [the longest x1 7.53 us: local(): jnp.dot(integrals, aux_half, preferred_element_type=jnp.float32)]
    unnamed x4 -> x10, local copies, waits for them, and re-layouts: 0.01 us -> 7.92 us
    gather x2 -> x0, local copies, waits for them, and re-layouts: 1.61 us -> none  [the longest x1 0.81 us: local(): jnp.diagonal(products)]
    sub x1 -> x0, other arithmetic: 1.61 us -> none  [local(): residual_rows = sigma_rows - own_trial * rayleigh[None, :]]
  transfers between devices with their start and end apart: 1 -> 0, of which waited for: 1 -> 0; matrix products, arithmetic and copies ran while one was open for 1% -> 0% of each run, Pallas kernels for 0% -> 0%
where the time goes in v1:
time: 44.7 us; the launch traced here: 44.4 us
  Pallas kernels  35.8 us (80%)
  local copies, waits for them, and re-layouts  7.92 us (18%)
  between operations  0.65 us (1%)
    pallas_call x1, Pallas kernels, local(): pl.pallas_call(functools.partial(kernel, np_, na, chunks, width, share),...  35.8 us
    unnamed x10, local copies, waits for them, and re-layouts  7.92 us

profile of v1, /device:TPU:0, one launch (start us, length us, event | category | flops | bytes accessed | tf_op | source)
XLA Modules:
  0.0 44.4 jit_solution(13991383342251257542)
XLA Ops:
  0.6 0.0 copy-start
  0.6 3.7 %copy-done = bf16[3072,1536]{1,0:T(8,128)(2,1)S(1)} copy-done((bf16[3072,1536]{1,0:T(8,128)(2,1)S(1)}, bf16[3072,1536]{1,0:T(8,128)(2,1)}, u32[]{:S(2)}) %copy-start) | copy-done | bytes 9437208
  4.3 0.0 copy-start.1
  4.3 1.1 %copy-done.1 = f32[3072,64]{0,1:T(8,128)S(1)} copy-done((f32[3072,64]{0,1:T(8,128)S(1)}, f32[3072,64]{0,1:T(8,128)}, u32[]{:S(2)}) %copy-start.1) | copy-done | bytes 786456
  5.4 0.0 copy-start.2
  5.4 0.7 %copy-done.2 = f32[3072]{0:T(1024)S(1)} copy-done((f32[3072]{0:T(1024)S(1)}, f32[3072]{0:T(1024)}, u32[]{:S(2)}) %copy-start.2) | copy-done | bytes 12312
  6.2 35.8 %sigma_build.1 = (f32[64,384]{1,0:T(8,128)S(1)}, f32[64,64]{1,0:T(8,128)S(1)}, f32[64,384]{1,0:T(8,128)S(1)}, f32[1,64]{1,0:T(1,128)S(1)}) custom-call(bf16[3072,1536]{1,0:T(8,128)(2,1)S(1)} %copy-done, f32[24,128]{1,0:T(8,128)S(1)} %bitcast.8, f32[64,3072]{1,0:T(8,128)S(1)} %bitcast.5), custom_call_target="tpu_custom_call" | custom-call | tf_op jit(solution)/shard_map/sigma_build/pallas_call | solution.py:303
  42.0 0.6 %copy.11 = f32[384,64]{0,1:T(8,128)} copy(f32[384,64]{0,1:T(8,128)S(1)} %bitcast.7) | data formatting | bytes 196608
  42.6 0.6 %copy.12 = f32[64,64]{1,0:T(8,128)} copy(f32[64,64]{1,0:T(8,128)S(1)} %get-tuple-element.17) | data formatting | bytes 32768
  43.3 0.6 %copy.13 = f32[384,64]{0,1:T(8,128)} copy(f32[384,64]{0,1:T(8,128)S(1)} %bitcast.6) | data formatting | bytes 196608
  43.9 0.5 %copy.14 = f32[64]{0:T(128)} copy(f32[64]{0:T(128)S(1)} %bitcast.9) | data formatting | bytes 512
Async XLA Ops:
  0.6 3.7 %copy-start = (bf16[3072,1536]{1,0:T(8,128)(2,1)S(1)}, bf16[3072,1536]{1,0:T(8,128)(2,1)}, u32[]{:S(2)}) copy-start(bf16[3072,1536]{1,0:T(8,128)(2,1)} %ints_hbm.1) | copy-start | bytes 28311556
  4.3 1.1 %copy-start.1 = (f32[3072,64]{0,1:T(8,128)S(1)}, f32[3072,64]{0,1:T(8,128)}, u32[]{:S(2)}) copy-start(f32[3072,64]{0,1:T(8,128)} %param.5) | copy-start | bytes 2359300
  5.4 0.7 %copy-start.2 = (f32[3072]{0:T(1024)S(1)}, f32[3072]{0:T(1024)}, u32[]{:S(2)}) copy-start(f32[3072]{0:T(1024)} %param.4) | copy-start | bytes 36868

commit v2 on v1

--- a/solution.py
+++ b/solution.py
@@ -10,7 +10,9 @@
 epsilon = 1e-06
 MESH = pl.DeviceIdType.MESH
 f32, bf16 = jnp.float32, jnp.bfloat16
-LAG = 2
+WIDTH = 256
+VMEM = 67043328
+LAG = 3
 NT = (((1,), (1,)), ((), ()))
 
 
@@ -288,6 +290,11 @@
         copy.wait()
 
 
+def store_kernel(*refs):
+    for i in range(4):
+        refs[i + 4][...] = refs[i][...]
+
+
 def solution(mesh):
     np_, na = mesh.shape["pair"], mesh.shape["aux"]
     chips = na // 2
@@ -295,12 +302,12 @@
     def local(integrals, energy_gaps, trial_vectors):
         rows, cols = integrals.shape
         vecs = trial_vectors.shape[1]
-        width = 256
+        width = WIDTH
         chunks, share = cols // width, rows // na
         anywhere = pl.BlockSpec(memory_space=pl.ANY)
         dma = pltpu.SemaphoreType.DMA
         message = (vecs // 2 + 8, 2 * vecs)
-        sigma, subspace, residuals, norms = pl.pallas_call(
+        results = pl.pallas_call(
             functools.partial(kernel, np_, na, chunks, width, share),
             out_shape=[
                 jax.ShapeDtypeStruct((vecs, share), f32),
@@ -308,7 +315,7 @@
                 jax.ShapeDtypeStruct((vecs, share), f32),
                 jax.ShapeDtypeStruct((1, vecs), f32),
             ],
-            in_specs=[pl.BlockSpec(memory_space=pltpu.HBM)] * 3,
+            in_specs=[anywhere] * 3,
             out_specs=[anywhere] * 4,
             scratch_shapes=[
                 pltpu.VMEM((chunks, rows, width), bf16),
@@ -339,10 +346,18 @@
                 dma((4,)),
             ],
             compiler_params=pltpu.CompilerParams(
-                collective_id=0, has_side_effects=True, vmem_limit_bytes=40 * 1024 * 1024
+                collective_id=0, has_side_effects=True, vmem_limit_bytes=VMEM
             ),
             name="sigma_build",
         )(integrals, energy_gaps.reshape(rows // 128, 128), trial_vectors.T)
+        sigma, subspace, residuals, norms = pl.pallas_call(
+            store_kernel,
+            out_shape=[jax.ShapeDtypeStruct(x.shape, x.dtype) for x in results],
+            in_specs=[pl.BlockSpec(memory_space=pltpu.VMEM)] * 4,
+            out_specs=[pl.BlockSpec(memory_space=pltpu.VMEM)] * 4,
+            compiler_params=pltpu.CompilerParams(vmem_limit_bytes=VMEM),
+            name="store",
+        )(*results)
         return sigma.T, subspace, residuals.T, norms.reshape(vecs)
 
     return jax.shard_map(

time: 44.7 us -> 37.9 us (0.85)
  local copies, waits for them, and re-layouts: 7.92 us -> 0 us
  Pallas kernels: 35.8 us -> 37.1 us
    unnamed x10 -> x0, local copies, waits for them, and re-layouts: 7.92 us -> none
    pallas_call x0 -> x1, Pallas kernels: none -> 1.65 us  [local(): pl.pallas_call(store_kernel, out_shape=[jax.ShapeDtypeStruct(x.shape, x.d...]
where the time goes in v2:
time: 37.9 us; the launch traced here: 37.8 us
  Pallas kernels  37.1 us (98%)
  between operations  0.64 us (2%)
    pallas_call x1, Pallas kernels, local(): pl.pallas_call(functools.partial(kernel, np_, na, chunks, width, share),...  35.5 us
    pallas_call x1, Pallas kernels, local(): pl.pallas_call(store_kernel, out_shape=[jax.ShapeDtypeStruct(x.shape, x.d...  1.65 us

profile of v2, /device:TPU:0, one launch (start us, length us, event | category | flops | bytes accessed | tf_op | source)
XLA Modules:
  0.0 37.8 jit_solution(18129522142780015815)
XLA Ops:
  0.6 35.5 %sigma_build.1 = (f32[64,384]{1,0:T(8,128)}, f32[64,64]{1,0:T(8,128)}, f32[64,384]{1,0:T(8,128)}, f32[1,64]{1,0:T(1,128)}) custom-call(bf16[3072,1536]{1,0:T(8,128)(2,1)} %ints_hbm.1, f32[24,128]{1,0:T(8,128)} %bitcast.6, f32[64,3072]{1,0:T(8,128)} %bitcast.5), custom_call_target="tpu_custom_call" | custom-call | tf_op jit(solution)/shard_map/sigma_build/pallas_call | solution.py:310
  36.1 1.7 %store.1 = (f32[64,384]{1,0:T(8,128)}, f32[64,64]{1,0:T(8,128)}, f32[64,384]{1,0:T(8,128)}, f32[1,64]{1,0:T(1,128)}) custom-call(f32[64,384]{1,0:T(8,128)} %get-tuple-element.12.refs_0_, f32[64,64]{1,0:T(8,128)} %get-tuple-element.13.refs_1_, f32[64,384]{1,0:T(8,128)} %get-tuple-element.14.refs_2_, f32[1,64]{1,0:T(1,128)} %get-tuple-element.15.refs_3_), custom_call_target="tpu_custom_call" | custom-call | tf_op jit(solution)/shard_map/store/pallas_call | solution.py:353
